TPU v7x, 32 devices: a whole 2x2x4 slice. The times are simulated.
32 devices in a mesh: expert: 4 (over x, core), shard: 8 (over z, y).
Axes of the slice: x: 2, y: 2, z: 4, core: 2. Of those that a mesh axis runs over, the one named last changes fastest.
Arguments:
- master_gate: float32 [64, 2048, 1024], P('expert', 'shard'), may hold values from -0.1875 to 0.1875
- master_up: float32 [64, 2048, 1024], P('expert', 'shard'), may hold values from -0.1875 to 0.1875
- master_down: float32 [64, 1024, 2048], P('expert', None, 'shard'), may hold values from -0.25 to 0.25
- router_weight: float32 [2048, 64], P('shard', 'expert'), may hold values from -0.125 to 0.125
- router_gain: float32 [2048], P('shard'), may hold values from 0.25 to 1.75
Outputs:
- final_gate: bfloat16 [64, 2048, 1024], P('expert', None, 'shard')
- final_up: bfloat16 [64, 2048, 1024], P('expert', None, 'shard')
- final_down: bfloat16 [64, 1024, 2048], P('expert', 'shard')
- scale_gate: float32 [64, 1024], P('expert', 'shard')
- scale_up: float32 [64, 1024], P('expert', 'shard')
- scale_down: float32 [64, 1024], P('expert', 'shard')
- serve_router: bfloat16 [2048, 64], replicated
All inputs are finite; a program needn't handle non-finite values.
Results may differ from a plain program's by a relative error of at most 0.001.
Values may be sent and summed in bfloat16 or wider, within the bound.
A program may use at most 192 MiB of HBM per device.

v0:
```python
import jax
import jax.numpy as jnp
from jax import lax
from jax.sharding import PartitionSpec as P


def on_device(master_gate, master_up, master_down, router_weight, router_gain):
    total_gate, total_up, total_down = lax.psum(
        (
            jnp.sum(master_gate * master_gate, axis=1),
            jnp.sum(master_up * master_up, axis=1),
            jnp.sum(master_down * master_down, axis=2),
        ),
        "shard",
    )
    scale_gate = jnp.sqrt(total_gate)
    scale_up = jnp.sqrt(total_up)
    scale_down = jnp.sqrt(total_down)
    narrow_gate, narrow_up, narrow_down = (
        (master_gate / jnp.expand_dims(scale_gate, 1)).astype(jnp.bfloat16),
        (master_up / jnp.expand_dims(scale_up, 1)).astype(jnp.bfloat16),
        (master_down / jnp.expand_dims(scale_down, 2)).astype(jnp.bfloat16),
    )
    final_gate, final_up = (
        lax.all_to_all(narrow_gate, "shard", split_axis=2, concat_axis=1, tiled=True),
        lax.all_to_all(narrow_up, "shard", split_axis=2, concat_axis=1, tiled=True),
    )
    final_down = lax.all_to_all(narrow_down, "shard", split_axis=1, concat_axis=2, tiled=True)
    scale_gate = lax.dynamic_slice_in_dim(
        scale_gate, lax.axis_index("shard") * final_gate.shape[2], final_gate.shape[2], axis=1
    )
    scale_up = lax.dynamic_slice_in_dim(
        scale_up, lax.axis_index("shard") * final_up.shape[2], final_up.shape[2], axis=1
    )
    scale_down = lax.dynamic_slice_in_dim(
        scale_down, lax.axis_index("shard") * final_down.shape[1], final_down.shape[1], axis=1
    )
    part_router = (router_weight * router_gain[:, None]).astype(jnp.bfloat16)
    row_router = lax.all_gather(part_router, "shard", axis=0, tiled=True)
    serve_router = lax.all_gather(row_router, "expert", axis=1, tiled=True)
    return (final_gate, final_up, final_down, scale_gate, scale_up, scale_down, serve_router)


def solution(mesh):
    placed = (
        P("expert", "shard", None),
        P("expert", "shard", None),
        P("expert", None, "shard"),
        P("shard", "expert"),
        P("shard"),
    )
    return jax.shard_map(
        on_device,
        mesh=mesh,
        in_specs=placed,
        out_specs=(
            P("expert", None, "shard"),
            P("expert", None, "shard"),
            P("expert", "shard", None),
            P("expert", "shard"),
            P("expert", "shard"),
            P("expert", "shard"),
            P(),
        ),
        check_vma=False,
    )
```

profile of v0, /device:TPU:0, one launch (start us, length us, event | category | flops | bytes accessed | tf_op | source)
XLA Modules:
  0.0 758.6 jit_solution(1279384502401970627)
XLA Ops:
  7.2 0.0 all-reduce.3.cloned.1.call-start
  7.2 8.6 %multiply_reduce_fusion = f32[16,1024]{1,0:T(8,128)} fusion(f32[16,1024,256]{2,1,0:T(8,128)} %param.7), kind=kLoop, calls=%fused_computation.2 | loop fusion | flops 8372224 | bytes 16842752 | tf_op jit(solution)/shard_map/reduce_sum | solution.py:12
  15.8 12.6 %multiply_reduce_fusion.1 = (f32[16,1024]{1,0:T(8,128)}, f32[16,1024]{1,0:T(8,128)}) fusion(f32[16,256,1024]{2,1,0:T(8,128)} %param.6, f32[16,256,1024]{2,1,0:T(8,128)} %param.5), kind=kLoop, calls=%fused_computation.4 | loop fusion | flops 16744448 | bytes 33685504 | tf_op jit(solution)/shard_map/reduce_sum | solution.py:11
  28.4 0.0 all-reduce.3.cloned.1.call-update
  28.4 17.6 %copy.19 = f32[16,256,1024]{1,0,2:T(8,128)} copy(f32[16,256,1024]{2,1,0:T(8,128)} %param.6) | data formatting | bytes 33554432 | tf_op args[1]
  46.0 56.7 %all-reduce.3.cloned.1.call-done = (f32[16,1024]{1,0:T(8,128)}, f32[16,1024]{1,0:T(8,128)}, f32[16,1024]{1,0:T(8,128)}) async-done(((f32[16,1024]{1,0:T(8,128)}, f32[16,1024]{1,0:T(8,128)}, f32[16,1024]{1,0:T(8,128)}), (f32[16,1024]{1,0:T(8,128)}, f32[16,1024]{1,0:T(8,128)}, f32[16,1024]{1,0:T(8,128)})) %all-reduce.3.cloned.1.call-update) | async-done | bytes 196624 | tf_op jit(solution)/shard_map/psum | solution.py:8
  102.7 0.9 sqrt.10
  103.6 0.2 copy.18
  103.8 9.6 %divide_convert_fusion = bf16[16,256,1024]{1,0,2:T(8,128)(2,1)} fusion(f32[16,256,1024]{1,0,2:T(8,128)} %copy.19, f32[16,1024]{0,1:T(8,128)S(1)} %copy.18), kind=kLoop, calls=%fused_computation.3 | loop fusion | flops 8388608 | bytes 25231360 | tf_op jit(solution)/shard_map/convert_element_type | solution.py:21
  113.4 4.9 all-to-all-start.1
  118.4 0.0 copy-start.1
  118.4 17.6 %copy.16 = f32[16,256,1024]{1,0,2:T(8,128)} copy(f32[16,256,1024]{2,1,0:T(8,128)} %param.5) | data formatting | bytes 33554432 | tf_op args[0]
  136.0 0.0 copy-done.1
  136.0 0.2 copy.15
  136.2 0.0 copy-start
  136.2 9.7 %divide_convert_fusion.1 = bf16[16,256,1024]{1,0,2:T(8,128)(2,1)} fusion(f32[16,256,1024]{1,0,2:T(8,128)} %copy.16, f32[16,1024]{0,1:T(8,128)S(1)} %copy.15), kind=kLoop, calls=%fused_computation.5 | loop fusion | flops 8388608 | bytes 25231360 | tf_op jit(solution)/shard_map/convert_element_type | solution.py:20
  145.9 153.8 %all-to-all-done.1 = bf16[16,256,1024]{1,0,2:T(8,128)(2,1)} async-done(((bf16[16,256,1024]{1,0,2:T(8,128)(2,1)}), bf16[16,256,1024]{1,0,2:T(8,128)(2,1)}, u32[]{:S(2)}, u32[]{:S(2)}) %all-to-all-start.1) | async-done | bytes 8388640 | tf_op jit(solution)/shard_map/all_to_all | solution.py:26
  299.7 4.9 all-to-all-start
  304.7 0.0 copy-done
  304.7 0.2 copy.21
  304.9 0.0 copy-start.2
  304.9 0.0 copy-start.3
  305.0 16.6 %fusion = bf16[16,1024,256]{2,0,1:T(8,128)(2,1)} fusion(f32[16,1024,256]{2,1,0:T(8,128)} %param.7, f32[16,1024]{0,1:T(8,128)S(1)} %copy.21), kind=kLoop, calls=%fused_computation.1 | loop fusion | flops 8388608 | bytes 25231360 | tf_op jit(solution)/shard_map/convert_element_type | solution.py:22
  321.6 165.1 %all-to-all-done = bf16[16,256,1024]{1,0,2:T(8,128)(2,1)} async-done(((bf16[16,256,1024]{1,0,2:T(8,128)(2,1)}), bf16[16,256,1024]{1,0,2:T(8,128)(2,1)}, u32[]{:S(2)}, u32[]{:S(2)}) %all-to-all-start) | async-done | bytes 8388640 | tf_op jit(solution)/shard_map/all_to_all | solution.py:25
  486.7 5.0 all-to-all-start.2
  491.7 0.0 copy-done.2
  491.8 0.0 copy-done.3
  491.8 202.1 %all_gather.6 = bf16[2048,16]{0,1:T(8,128)(2,1)S(1)} all-gather(bf16[256,16]{0,1:T(8,128)(2,1)S(1)} %multiply_convert_fusion), channel_id=1, replica_groups=mesh['expert'=4,'shard'=8] {'shard'}, dimensions={0}, use_global_device_ids=true | all-gather | bytes 73728 | tf_op jit(solution)/shard_map/all_gather | solution.py:39
  693.9 5.9 all_gather.7
  699.9 0.6 constant_dynamic-slice_fusion
  700.5 0.6 constant_dynamic-slice_fusion.1
  701.1 0.6 constant_dynamic-slice_fusion.2
  701.7 12.3 %copy.20 = bf16[16,8,256,128]{3,2,1,0:T(8,128)(2,1)} copy(bf16[16,8,256,128]{2,0,3,1:T(8,128)(2,1)} %bitcast.4) | data formatting | bytes 16777216 | tf_op jit(solution)/shard_map/all_to_all | solution.py:26
  713.9 12.3 %copy.17 = bf16[16,8,256,128]{3,2,1,0:T(8,128)(2,1)} copy(bf16[16,8,256,128]{2,0,3,1:T(8,128)(2,1)} %bitcast.1) | data formatting | bytes 16777216 | tf_op jit(solution)/shard_map/all_to_all | solution.py:25
  726.2 0.0 all-to-all-done.2
  726.2 11.4 %copy.23 = bf16[16,128,8,256]{3,2,1,0:T(8,128)(2,1)} copy(bf16[16,128,8,256]{3,0,1,2:T(8,128)(2,1)} %bitcast.7) | data formatting | bytes 16777216 | tf_op jit(solution)/shard_map/all_to_all | solution.py:28
  737.6 13.4 %all_to_all.50 = bf16[16,128,2048]{2,1,0:T(8,128)(2,1)} reshape(bf16[16,128,8,256]{3,2,1,0:T(8,128)(2,1)} %copy.23) | data formatting | bytes 16777216 | tf_op jit(solution)/shard_map/all_to_all | solution.py:28
  751.0 0.7 copy.31
  (3 shorter events, 0.0 us)
Async XLA Ops:
  7.2 95.5 %all-reduce.3.cloned.1.call-start = ((), (), s32[]{:S(2)}) async-start(), calls=%async_computation.3 | async-start | bytes 393216 | tf_op jit(solution)/shard_map/psum | solution.py:8
  113.4 186.3 %all-to-all-start.1 = ((bf16[16,256,1024]{1,0,2:T(8,128)(2,1)}), bf16[16,256,1024]{1,0,2:T(8,128)(2,1)}, u32[]{:S(2)}, u32[]{:S(2)}) async-start(bf16[16,256,1024]{1,0,2:T(8,128)(2,1)} %divide_convert_fusion), calls=%async_computation.1 | async-start | bytes 16777216 | tf_op jit(solution)/shard_map/all_to_all | solution.py:26
  118.4 17.6 %copy-start.1 = (f32[16,1024]{1,0:T(8,128)S(1)}, f32[16,1024]{1,0:T(8,128)}, u32[]{:S(2)}) copy-start(f32[16,1024]{1,0:T(8,128)} %get-tuple-element.7) | copy-start | bytes 196612
  136.2 168.5 %copy-start = (f32[16,1024]{1,0:T(8,128)S(1)}, f32[16,1024]{1,0:T(8,128)}, u32[]{:S(2)}) copy-start(f32[16,1024]{1,0:T(8,128)} %get-tuple-element.9) | copy-start | bytes 196612
  299.7 187.0 %all-to-all-start = ((bf16[16,256,1024]{1,0,2:T(8,128)(2,1)}), bf16[16,256,1024]{1,0,2:T(8,128)(2,1)}, u32[]{:S(2)}, u32[]{:S(2)}) async-start(bf16[16,256,1024]{1,0,2:T(8,128)(2,1)} %divide_convert_fusion.1), calls=%async_computation | async-start | bytes 16777216 | tf_op jit(solution)/shard_map/all_to_all | solution.py:25
  304.9 186.8 %copy-start.2 = (f32[256,16]{0,1:T(8,128)S(1)}, f32[256,16]{0,1:T(8,128)}, u32[]{:S(2)}) copy-start(f32[256,16]{0,1:T(8,128)} %param.8) | copy-start | bytes 49156
  304.9 186.8 %copy-start.3 = (f32[256]{0:T(256)S(1)}, f32[256]{0:T(256)}, u32[]{:S(2)}) copy-start(f32[256]{0:T(256)} %param.9) | copy-start | bytes 3076
  486.7 239.5 %all-to-all-start.2 = ((bf16[16,1024,256]{2,0,1:T(8,128)(2,1)}), bf16[16,1024,256]{2,0,1:T(8,128)(2,1)}, u32[]{:S(2)}, u32[]{:S(2)}) async-start(bf16[16,1024,256]{2,0,1:T(8,128)(2,1)} %fusion), calls=%async_computation.2 | async-start | bytes 16777216 | tf_op jit(solution)/shard_map/all_to_all | solution.py:28
Sparse Core Ops, SparseCore 0:
  28.6 74.0 all-reduce.2
where the time goes:
time: 760 us; the launch traced here: 759 us
  waiting for transfers between devices  376 us (49%)
  blocking collectives  208 us (27%)
  local copies, waits for them, and re-layouts  88.6 us (12%)
  other arithmetic  57.2 us (8%)
  starting transfers between devices  14.9 us (2%)
  between operations  14.2 us (2%)
    all_gather x1, blocking collectives, on_device(): row_router = lax.all_gather(part_router, 'shard', axis=0, tiled=True)  202 us
    all_to_all x1, waiting for transfers between devices, on_device(): lax.all_to_all(narrow_gate, 'shard', split_axis=2, concat_axis=1, tiled=T...  165 us
    all_to_all x1, waiting for transfers between devices, on_device(): lax.all_to_all(narrow_up, 'shard', split_axis=2, concat_axis=1, tiled=True)  154 us
    psum x1, waiting for transfers between devices, on_device(): lax.psum((jnp.sum(master_gate * master_gate, axis=1), jnp.sum(master_up *...  56.7 us
    unnamed x11, local copies, waits for them, and re-layouts  35.9 us
    all_to_all x2, local copies, waits for them, and re-layouts, on_device(): lax.all_to_all(narrow_down, 'shard', split_axis=1, concat_axis=2, tiled=T...  24.8 us
    convert_element_type x1, other arithmetic, on_device(): (master_down / jnp.expand_dims(scale_down, 2)).astype(jnp.bfloat16)  16.6 us
  transfers between devices with their start and end apart: 4, of which 3 were waited for; matrix products, arithmetic and copies ran while one was open for 12% of the time, Pallas kernels for 0%

commit v1 on v0

--- a/solution.py
+++ b/solution.py
@@ -2,6 +2,18 @@
 import jax.numpy as jnp
 from jax import lax
 from jax.sharding import PartitionSpec as P
+
+
+def expand_blocks(xs, net_axis):
+    return jnp.concatenate(
+        jax.lax.all_to_all(
+            jnp.stack(jnp.split(xs, jax.lax.axis_size(net_axis), axis=2)),
+            axis_name=net_axis,
+            split_axis=0,
+            concat_axis=0,
+        ),
+        axis=1,
+    )
 
 
 def on_device(master_gate, master_up, master_down, router_weight, router_gain):
@@ -23,7 +35,7 @@
     )
     final_gate, final_up = (
         lax.all_to_all(narrow_gate, "shard", split_axis=2, concat_axis=1, tiled=True),
-        lax.all_to_all(narrow_up, "shard", split_axis=2, concat_axis=1, tiled=True),
+        expand_blocks(narrow_up, "shard"),
     )
     final_down = lax.all_to_all(narrow_down, "shard", split_axis=1, concat_axis=2, tiled=True)
     scale_gate = lax.dynamic_slice_in_dim(

time: 760 us -> 756 us (level)
  local copies, waits for them, and re-layouts: 88.6 us -> 76.3 us
  waiting for transfers between devices: 376 us -> 386 us
    all_to_all x1 -> x0, local copies, waits for them, and re-layouts: 12.3 us -> none  [on_device(): lax.all_to_all(narrow_up, 'shard', split_axis=2, concat_axis=1, tiled=True)]
    all_to_all x1, waiting for transfers between devices: 154 us -> 165 us  [expand_blocks(): jax.lax.all_to_all(jnp.stack(jnp.split(xs, jax.lax.axis_size(net_axis), a...]
    unnamed x11 -> x17, local copies, waits for them, and re-layouts: 35.9 us -> 27 us
    reshape x0 -> x1, local copies, waits for them, and re-layouts: none -> 7.89 us  [expand_blocks(): jnp.concatenate(jax.lax.all_to_all(jnp.stack(jnp.split(xs, jax.lax.axis_s...]
  transfers between devices with their start and end apart: 4 -> 4, of which waited for: 3 -> 3; matrix products, arithmetic and copies ran while one was open for 12% -> 10% of each run, Pallas kernels for 0% -> 0%
where the time goes in v1:
time: 756 us; the launch traced here: 754 us
  waiting for transfers between devices  386 us (51%)
  blocking collectives  208 us (28%)
  local copies, waits for them, and re-layouts  76.3 us (10%)
  other arithmetic  54.7 us (7%)
  starting transfers between devices  15.2 us (2%)
  between operations  14.2 us (2%)
    all_gather x1, blocking collectives, on_device(): row_router = lax.all_gather(part_router, 'shard', axis=0, tiled=True)  202 us
    all_to_all x1, waiting for transfers between devices, expand_blocks(): jax.lax.all_to_all(jnp.stack(jnp.split(xs, jax.lax.axis_size(net_axis), a...  165 us
    all_to_all x1, waiting for transfers between devices, on_device(): lax.all_to_all(narrow_gate, 'shard', split_axis=2, concat_axis=1, tiled=T...  164 us
    psum x1, waiting for transfers between devices, on_device(): lax.psum((jnp.sum(master_gate * master_gate, axis=1), jnp.sum(master_up *...  56.7 us
    unnamed x17, local copies, waits for them, and re-layouts  27 us
    all_to_all x2, local copies, waits for them, and re-layouts, on_device(): lax.all_to_all(narrow_down, 'shard', split_axis=1, concat_axis=2, tiled=T...  24.8 us
    convert_element_type x1, other arithmetic, on_device(): (master_down / jnp.expand_dims(scale_down, 2)).astype(jnp.bfloat16)  16.6 us
  transfers between devices with their start and end apart: 4, of which 3 were waited for; matrix products, arithmetic and copies ran while one was open for 10% of the time, Pallas kernels for 0%

profile of v1, /device:TPU:0, one launch (start us, length us, event | category | flops | bytes accessed | tf_op | source)
XLA Modules:
  0.0 754.3 jit_solution(11293946100042297443)
XLA Ops:
  7.2 0.0 all-reduce.3.cloned.1.call-start
  7.2 8.6 %multiply_reduce_fusion = f32[16,1024]{1,0:T(8,128)} fusion(f32[16,1024,256]{2,1,0:T(8,128)} %param.7), kind=kLoop, calls=%fused_computation.2 | loop fusion | flops 8372224 | bytes 16842752 | tf_op jit(solution)/shard_map/reduce_sum | solution.py:24
  15.8 12.6 %multiply_reduce_fusion.1 = (f32[16,1024]{1,0:T(8,128)}, f32[16,1024]{1,0:T(8,128)}) fusion(f32[16,256,1024]{2,1,0:T(8,128)} %param.6, f32[16,256,1024]{2,1,0:T(8,128)} %param.5), kind=kLoop, calls=%fused_computation.4 | loop fusion | flops 16744448 | bytes 33685504 | tf_op jit(solution)/shard_map/reduce_sum | solution.py:23
  28.4 0.0 all-reduce.3.cloned.1.call-update
  28.4 17.6 %copy.16 = f32[16,256,1024]{1,0,2:T(8,128)} copy(f32[16,256,1024]{2,1,0:T(8,128)} %param.5) | data formatting | bytes 33554432 | tf_op args[0]
  46.0 56.7 %all-reduce.3.cloned.1.call-done = (f32[16,1024]{1,0:T(8,128)}, f32[16,1024]{1,0:T(8,128)}, f32[16,1024]{1,0:T(8,128)}) async-done(((f32[16,1024]{1,0:T(8,128)}, f32[16,1024]{1,0:T(8,128)}, f32[16,1024]{1,0:T(8,128)}), (f32[16,1024]{1,0:T(8,128)}, f32[16,1024]{1,0:T(8,128)}, f32[16,1024]{1,0:T(8,128)})) %all-reduce.3.cloned.1.call-update) | async-done | bytes 196624 | tf_op jit(solution)/shard_map/psum | solution.py:20
  102.7 0.9 sqrt.9
  103.6 0.2 copy.15
  103.8 9.6 %divide_convert_fusion.1 = bf16[16,256,1024]{1,0,2:T(8,128)(2,1)} fusion(f32[16,256,1024]{1,0,2:T(8,128)} %copy.16, f32[16,1024]{0,1:T(8,128)S(1)} %copy.15), kind=kLoop, calls=%fused_computation.5 | loop fusion | flops 8388608 | bytes 25231360 | tf_op jit(solution)/shard_map/convert_element_type | solution.py:32
  113.4 0.0 copy-start.1
  113.4 5.1 all-to-all-start
  118.5 0.0 copy-done.1
  118.5 7.2 divide_convert_fusion
  125.8 1.2 fusion.8
  127.0 1.2 fusion.7
  128.3 1.2 fusion.6
  129.5 1.2 fusion.5
  130.8 1.2 fusion.4
  132.0 1.2 fusion.3
  133.3 1.2 fusion.2
  134.5 1.2 fusion.1
  135.8 0.0 copy-start
  135.8 164.1 %all-to-all-done = bf16[16,256,1024]{1,0,2:T(8,128)(2,1)} async-done(((bf16[16,256,1024]{1,0,2:T(8,128)(2,1)}), bf16[16,256,1024]{1,0,2:T(8,128)(2,1)}, u32[]{:S(2)}, u32[]{:S(2)}) %all-to-all-start) | async-done | bytes 8388640 | tf_op jit(solution)/shard_map/all_to_all | solution.py:37
  299.9 5.0 all-to-all-start.1
  304.9 0.0 copy-done
  304.9 0.2 copy.19
  305.1 16.6 %fusion = bf16[16,1024,256]{2,0,1:T(8,128)(2,1)} fusion(f32[16,1024,256]{2,1,0:T(8,128)} %param.7, f32[16,1024]{0,1:T(8,128)S(1)} %copy.19), kind=kLoop, calls=%fused_computation.1 | loop fusion | flops 8388608 | bytes 25231360 | tf_op jit(solution)/shard_map/convert_element_type | solution.py:34
  321.8 0.0 copy-start.2
  321.8 0.0 copy-start.3
  321.8 165.1 %all-to-all-done.1 = bf16[8,16,256,128]{3,2,1,0:T(8,128)(2,1)} async-done(((bf16[8,16,256,128]{3,2,1,0:T(8,128)(2,1)}), bf16[8,16,256,128]{3,2,1,0:T(8,128)(2,1)}, u32[]{:S(2)}, u32[]{:S(2)}) %all-to-all-start.1) | async-done | bytes 8388640 | tf_op jit(solution)/shard_map/all_to_all | solution.py:9
  486.8 5.1 all-to-all-start.2
  492.0 0.0 copy-done.2
  492.0 0.0 copy-done.3
  492.0 202.2 %all_gather.6 = bf16[2048,16]{0,1:T(8,128)(2,1)S(1)} all-gather(bf16[256,16]{0,1:T(8,128)(2,1)S(1)} %multiply_convert_fusion), channel_id=1, replica_groups=mesh['expert'=4,'shard'=8] {'shard'}, dimensions={0}, use_global_device_ids=true | all-gather | bytes 73728 | tf_op jit(solution)/shard_map/all_gather | solution.py:51
  694.2 5.8 all_gather.7
  700.0 0.6 constant_dynamic-slice_fusion.2
  700.6 0.6 constant_dynamic-slice_fusion.1
  701.2 0.6 constant_dynamic-slice_fusion
  701.8 12.3 %copy.17 = bf16[16,8,256,128]{3,2,1,0:T(8,128)(2,1)} copy(bf16[16,8,256,128]{2,0,3,1:T(8,128)(2,1)} %bitcast.1) | data formatting | bytes 16777216 | tf_op jit(solution)/shard_map/all_to_all | solution.py:37
  714.1 7.9 %copy.18 = bf16[16,8,256,128]{3,2,1,0:T(8,128)(2,1)} copy(bf16[16,8,256,128]{3,2,0,1:T(8,128)(2,1)} %bitcast.11) | data formatting | bytes 16777216 | tf_op jit(solution)/shard_map/reshape | solution.py:8
  721.9 0.0 all-to-all-done.2
  722.0 11.4 %copy.21 = bf16[16,128,8,256]{3,2,1,0:T(8,128)(2,1)} copy(bf16[16,128,8,256]{3,0,1,2:T(8,128)(2,1)} %bitcast.14) | data formatting | bytes 16777216 | tf_op jit(solution)/shard_map/all_to_all | solution.py:40
  733.3 13.4 %all_to_all.37 = bf16[16,128,2048]{2,1,0:T(8,128)(2,1)} reshape(bf16[16,128,8,256]{3,2,1,0:T(8,128)(2,1)} %copy.21) | data formatting | bytes 16777216 | tf_op jit(solution)/shard_map/all_to_all | solution.py:40
  746.7 0.7 copy.36
  (3 shorter events, 0.1 us)
Async XLA Ops:
  7.2 95.5 %all-reduce.3.cloned.1.call-start = ((), (), s32[]{:S(2)}) async-start(), calls=%async_computation.3 | async-start | bytes 393216 | tf_op jit(solution)/shard_map/psum | solution.py:20
  113.4 5.1 copy-start.1
  113.4 186.5 %all-to-all-start = ((bf16[16,256,1024]{1,0,2:T(8,128)(2,1)}), bf16[16,256,1024]{1,0,2:T(8,128)(2,1)}, u32[]{:S(2)}, u32[]{:S(2)}) async-start(bf16[16,256,1024]{1,0,2:T(8,128)(2,1)} %divide_convert_fusion.1), calls=%async_computation | async-start | bytes 16777216 | tf_op jit(solution)/shard_map/all_to_all | solution.py:37
  135.8 169.1 %copy-start = (f32[16,1024]{1,0:T(8,128)S(1)}, f32[16,1024]{1,0:T(8,128)}, u32[]{:S(2)}) copy-start(f32[16,1024]{1,0:T(8,128)} %get-tuple-element.9) | copy-start | bytes 196612
  299.9 187.0 %all-to-all-start.1 = ((bf16[8,16,256,128]{3,2,1,0:T(8,128)(2,1)}), bf16[8,16,256,128]{3,2,1,0:T(8,128)(2,1)}, u32[]{:S(2)}, u32[]{:S(2)}) async-start(bf16[8,16,256,128]{3,2,1,0:T(8,128)(2,1)} %fusion.1), calls=%async_computation.1 | async-start | bytes 16777216 | tf_op jit(solution)/shard_map/all_to_all | solution.py:9
  321.8 170.2 %copy-start.2 = (f32[256,16]{0,1:T(8,128)S(1)}, f32[256,16]{0,1:T(8,128)}, u32[]{:S(2)}) copy-start(f32[256,16]{0,1:T(8,128)} %param.8) | copy-start | bytes 49156
  321.8 170.2 %copy-start.3 = (f32[256]{0:T(256)S(1)}, f32[256]{0:T(256)}, u32[]{:S(2)}) copy-start(f32[256]{0:T(256)} %param.9) | copy-start | bytes 3076
  486.8 235.1 %all-to-all-start.2 = ((bf16[16,1024,256]{2,0,1:T(8,128)(2,1)}), bf16[16,1024,256]{2,0,1:T(8,128)(2,1)}, u32[]{:S(2)}, u32[]{:S(2)}) async-start(bf16[16,1024,256]{2,0,1:T(8,128)(2,1)} %fusion), calls=%async_computation.2 | async-start | bytes 16777216 | tf_op jit(solution)/shard_map/all_to_all | solution.py:40
Sparse Core Ops, SparseCore 0:
  28.6 74.0 all-reduce.2
